TPU v7x, 32 devices: a whole 2x2x4 slice. The times are simulated.
32 devices in a mesh: section: 4 (over z), tensor: 4 (over y, x), dp: 2 (over core).
Axes of the slice: x: 2, y: 2, z: 4, core: 2. Of those that a mesh axis runs over, the one named last changes fastest.
Arguments:
- forward_rows: bfloat16 [4, 2, 192, 8192], P('section', 'dp', None, 'tensor'), may hold values from -6 to 6
- saved_rows: bfloat16 [4, 2, 192, 8192], P('section', 'dp', None, 'tensor'), may hold values from -40.5 to 40.5
- output_grad: bfloat16 [4, 2, 192, 8192], P('section', 'dp', None, 'tensor'), may hold values from -1.27 to 1.27
- lengths: int32 [4, 2, 2], P('section', 'dp'), may hold values from 1 to 96
- norm_gain: bfloat16 [4, 8192], P('section', 'tensor'), may hold values from 0.5 to 1.5
- down_map: bfloat16 [4, 192, 8192], P('section', None, 'tensor'), may hold values from -0.067396115 to 0.067396115
- up_map: bfloat16 [4, 192, 8192], P('section', None, 'tensor'), may hold values from -1.0625 to 1.0625
Outputs:
- next_inputs: bfloat16 [4, 2, 192, 8192], P('section', 'dp', None, 'tensor')
- next_grads: bfloat16 [4, 2, 192, 8192], P('section', 'dp', None, 'tensor')
- grad_down: bfloat16 [4, 192, 8192], P('section', 'dp', 'tensor')
- grad_up: bfloat16 [4, 192, 8192], P('section', 'dp', 'tensor')
All inputs are finite; a program needn't handle non-finite values.
Results may differ from a plain program's by a relative error of at most 0.02.
Values may be sent and summed in bfloat16 or wider, within the bound.
A program may use at most 64 MiB of HBM per device.

v0:
```python
import jax
import jax.numpy as jnp
from jax import lax
from jax.sharding import PartitionSpec as P

EPSILON = 1e-05


def padded_2(cells, sides, width):
    for axis, dim in sides:
        count = lax.axis_size(axis)
        ends = count - 1
        head = lax.slice_in_dim(cells, 0, width, axis=dim)
        tail = lax.slice_in_dim(cells, cells.shape[dim] - width, cells.shape[dim], axis=dim)
        cells = jnp.concatenate(
            [
                lax.ppermute(tail, axis, [(i, (i + 1) % count) for i in range(ends)]),
                cells,
                lax.ppermute(head, axis, [((i + 1) % count, i) for i in range(ends)]),
            ],
            axis=dim,
        )
    return cells


def contract_last(left_side, right_side):
    return lax.dot_general(
        left_side, right_side, (((1,), (1,)), ((), ())), preferred_element_type=jnp.float32
    )


def contract_rows(left_side, right_side):
    return lax.dot_general(
        left_side, right_side, (((0,), (0,)), ((), ())), preferred_element_type=jnp.float32
    )


def silu_slope(values):
    gate_value = jax.nn.sigmoid(values)
    return gate_value * (1.0 + values * (1.0 - gate_value))


def shards(forward_rows, saved_rows, output_grad, lengths, norm_gain, down_map, up_map):
    forward_block = forward_rows[0, 0]
    saved_block = saved_rows[0, 0]
    incoming = output_grad[0, 0]
    seq_lengths = lengths[0, 0]
    gain_cols = norm_gain[0].astype(jnp.float32)
    down_cols = down_map[0]
    up_cols = up_map[0]
    row_count = forward_block.shape[0]
    seq_rows = row_count // 2
    full_width = forward_block.shape[1] * lax.axis_size("tensor")
    forward_values = forward_block.astype(jnp.float32)
    saved_values = saved_block.astype(jnp.float32)
    forward_total, saved_total = lax.psum(
        (
            jnp.sum(forward_values * forward_values, axis=1),
            jnp.sum(saved_values * saved_values, axis=1),
        ),
        "tensor",
    )
    forward_scale = lax.rsqrt(forward_total / full_width + EPSILON)[:, None]
    saved_scale = lax.rsqrt(saved_total / full_width + EPSILON)[:, None]
    forward_normed = (forward_values * forward_scale * gain_cols).astype(jnp.bfloat16)
    saved_normed = (saved_values * saved_scale * gain_cols).astype(jnp.bfloat16)
    position = jnp.arange(row_count, dtype=jnp.int32)
    length_limit = jnp.where(position // seq_rows == 0, seq_lengths[0], seq_lengths[1])
    keep_rows = position % seq_rows < length_limit
    kept_grad = jnp.where(keep_rows[:, None], incoming, jnp.zeros_like(incoming))
    forward_part = contract_last(forward_normed, down_cols)
    saved_part = contract_last(saved_normed, down_cols)
    slope_part = contract_last(kept_grad, up_cols)
    forward_share, saved_share, slope_share = (
        lax.psum_scatter(
            forward_part.astype(jnp.bfloat16), "tensor", scatter_dimension=1, tiled=True
        ).astype(jnp.float32),
        lax.psum_scatter(
            saved_part.astype(jnp.bfloat16), "tensor", scatter_dimension=1, tiled=True
        ).astype(jnp.float32),
        lax.psum_scatter(
            slope_part.astype(jnp.bfloat16), "tensor", scatter_dimension=1, tiled=True
        ).astype(jnp.float32),
    )
    forward_act, saved_act, back_rank = (
        lax.all_gather(
            jax.nn.silu(forward_share).astype(jnp.bfloat16), "tensor", axis=1, tiled=True
        ),
        lax.all_gather(jax.nn.silu(saved_share).astype(jnp.bfloat16), "tensor", axis=1, tiled=True),
        lax.all_gather(
            (slope_share * silu_slope(saved_share)).astype(jnp.bfloat16),
            "tensor",
            axis=1,
            tiled=True,
        ),
    )
    forward_out = (
        forward_values + jnp.dot(forward_act, up_cols, preferred_element_type=jnp.float32)
    ).astype(jnp.bfloat16)
    back_normed = jnp.dot(back_rank, down_cols, preferred_element_type=jnp.float32)
    weighted = gain_cols * back_normed
    correction = lax.psum(jnp.sum(saved_values * weighted, axis=1), "tensor")[:, None] / full_width
    scale_cube = saved_scale * saved_scale * saved_scale
    grad_rows = (
        kept_grad.astype(jnp.float32)
        + saved_scale * weighted
        - saved_values * scale_cube * correction
    ).astype(jnp.bfloat16)
    section_edges = jnp.stack([grad_rows, forward_out], axis=0)
    padded = padded_2(section_edges, (("section", 0),), 1)
    down_part = contract_rows(back_rank, saved_normed)
    up_part = contract_rows(saved_act, kept_grad)
    down_sum, up_sum = (
        lax.psum_scatter(
            down_part.astype(jnp.bfloat16), "dp", scatter_dimension=0, tiled=True
        ).astype(jnp.float32),
        lax.psum_scatter(
            up_part.astype(jnp.bfloat16), "dp", scatter_dimension=0, tiled=True
        ).astype(jnp.float32),
    )
    mean_weight = 1.0 / lax.axis_size("dp")
    grad_down = (down_sum * mean_weight).astype(jnp.bfloat16)
    grad_up = (up_sum * mean_weight).astype(jnp.bfloat16)
    return (padded[0][None, None], padded[3][None, None], grad_down[None], grad_up[None])


def solution(mesh):
    placed = (
        P("section", "dp", None, "tensor"),
        P("section", "dp", None, "tensor"),
        P("section", "dp", None, "tensor"),
        P("section", "dp", None),
        P("section", "tensor"),
        P("section", None, "tensor"),
        P("section", None, "tensor"),
    )
    return jax.shard_map(
        shards,
        mesh=mesh,
        in_specs=placed,
        out_specs=(
            P("section", "dp", None, "tensor"),
            P("section", "dp", None, "tensor"),
            P("section", "dp", "tensor"),
            P("section", "dp", "tensor"),
        ),
        check_vma=False,
    )
```

profile of v0, /device:TPU:0, one launch (start us, length us, event | category | flops | bytes accessed | tf_op | source)
XLA Modules:
  0.0 157.6 jit_solution(3007640196093150440)
XLA Ops:
  8.0 1.4 fusion.10
  9.5 11.4 %psum.22 = f32[192]{0:T(256)S(1)} all-reduce(f32[192]{0:T(256)S(1)} %fusion.10), channel_id=1, replica_groups=mesh['section'=4,'tensor'=4,'dp'=2] {'tensor'}, use_global_device_ids=true, to_apply=%region_4.5 | all-reduce | flops 192 | bytes 1536 | tf_op jit(solution)/shard_map/psum | solution.py:56
  20.9 2.2 %convolution_convert_fusion.2 = bf16[192,192]{0,1:T(8,128)(2,1)} fusion(bf16[1,1,192,2048]{3,2,1,0:T(8,128)(2,1)} %param.8, bf16[1,192,2048]{2,1,0:T(8,128)(2,1)S(1)} %copy-done, f32[192]{0:T(256)S(1)} %get-tuple-element.9, f32[2048]{0:T(1024)S(1)} %bitcast.82), kind=kOutput, calls=%fused_computation.27 | convolution fusion | flops 152604672 | bytes 1655552 | tf_op jit(solution)/shard_map/dot_general | solution.py:27
  23.8 1.3 fusion.54
  25.1 2.3 %convolution_convert_fusion.3 = bf16[192,192]{0,1:T(8,128)(2,1)} fusion(bf16[1,192,2048]{2,1,0:T(8,128)(2,1)} %param.13, bf16[1,1,192,2048]{3,2,1,0:T(8,128)(2,1)S(1)} %copy-done.4, pred[192]{0:T(512)(128)(4,1)S(1)} %fusion.54), kind=kOutput, calls=%fused_computation.28 | convolution fusion | flops 151425024 | bytes 1646784 | tf_op jit(solution)/shard_map/dot_general | solution.py:27
  27.8 19.0 %reduce-scatter.10.cloned.1.call-done = bf16[192,48]{0,1:T(8,128)(2,1)} async-done(((bf16[192,192]{0,1:T(8,128)(2,1)}), bf16[192,48]{0,1:T(8,128)(2,1)}) %reduce-scatter.10.cloned.1.call-update) | async-done | bytes 18448 | tf_op jit(solution)/shard_map/reduce_scatter | solution.py:78
  46.8 27.5 %reduce-scatter.8.cloned.1.call-done = bf16[192,48]{0,1:T(8,128)(2,1)} async-done(((bf16[192,192]{0,1:T(8,128)(2,1)}), bf16[192,48]{0,1:T(8,128)(2,1)}) %reduce-scatter.8.cloned.1.call-update) | async-done | bytes 18448 | tf_op jit(solution)/shard_map/reduce_scatter | solution.py:81
  74.3 0.8 fusion.53
  75.1 8.3 %all_gather.10 = bf16[192,192]{0,1:T(8,128)(2,1)S(1)} all-gather(bf16[192,48]{0,1:T(8,128)(2,1)S(1)} %get-tuple-element.7), channel_id=1, replica_groups=mesh['section'=4,'tensor'=4,'dp'=2] {'tensor'}, dimensions={1}, use_global_device_ids=true | all-gather | bytes 92160 | tf_op jit(solution)/shard_map/all_gather | solution.py:90
  83.9 8.9 %all-reduce = (f32[192]{0:T(256)S(1)}, f32[192]{0:T(256)S(1)}) all-reduce(f32[192]{0:T(256)S(1)} %fusion.7, f32[192]{0:T(256)S(1)} %get-tuple-element.12), channel_id=1, replica_groups=mesh['section'=4,'tensor'=4,'dp'=2] {'tensor'}, use_global_device_ids=true, to_apply=%region_1.0 | all-reduce | flops 384 | bytes 3072 | tf_op jit(solution)/shard_map/psum | solution.py:56
  92.8 2.2 %convolution_convert_fusion.4 = bf16[192,192]{0,1:T(8,128)(2,1)} fusion(bf16[1,1,192,2048]{3,2,1,0:T(8,128)(2,1)} %param.7, bf16[1,192,2048]{2,1,0:T(8,128)(2,1)S(1)} %copy-done, f32[2048]{0:T(1024)S(1)} %bitcast.84, f32[192]{0:T(256)S(1)} %add_rsqrt_fusion.1), kind=kOutput, calls=%fused_computation.29 | convolution fusion | flops 152604672 | bytes 1655552 | tf_op jit(solution)/shard_map/dot_general | solution.py:27
  95.1 1.4 convolution_convert_fusion.1
  96.6 2.6 %fusion.22 = bf16[1,192,2048]{2,1,0:T(8,128)(2,1)} fusion(bf16[1,1,192,2048]{3,2,1,0:T(8,128)(2,1)S(1)} %copy-done.1, f32[192,2048]{1,0:T(8,128)S(1)} %get-tuple-element.13, f32[192]{0:T(256)S(1)} %broadcast_multiply_fusion, f32[192]{0:T(256)S(1)} %get-tuple-element.8, f32[192]{0:T(256)S(1)} %get-tuple-element.9, bf16[1,1,192,2048]{3,2,1,0:T(8,128)(2,1)} %param.9, ...), kind=kLoop, calls=%fused_computation.31 | loop fusion | flops 3538944 | bytes 3934656 | tf_op jit(solution)/shard_map/stack | solution.py:109
  99.2 1.4 collective-permute-start.1
  100.6 7.4 %all_gather.11 = bf16[192,192]{0,1:T(8,128)(2,1)S(1)} all-gather(bf16[192,48]{0,1:T(8,128)(2,1)S(1)} %get-tuple-element.6), channel_id=1, replica_groups=mesh['section'=4,'tensor'=4,'dp'=2] {'tensor'}, dimensions={1}, use_global_device_ids=true | all-gather | bytes 92160 | tf_op jit(solution)/shard_map/all_gather | solution.py:89
  108.0 1.3 convolution_convert_fusion
  109.4 9.1 %reduce-scatter.6.cloned.1.call-done = bf16[192,48]{0,1:T(8,128)(2,1)} async-done(((bf16[192,192]{0,1:T(8,128)(2,1)}), bf16[192,48]{0,1:T(8,128)(2,1)}) %reduce-scatter.6.cloned.1.call-update) | async-done | bytes 18448 | tf_op jit(solution)/shard_map/reduce_scatter | solution.py:75
  119.2 8.4 %all_gather.9 = bf16[192,192]{0,1:T(8,128)(2,1)S(1)} all-gather(bf16[192,48]{0,1:T(8,128)(2,1)S(1)} %fusion.45), channel_id=1, replica_groups=mesh['section'=4,'tensor'=4,'dp'=2] {'tensor'}, dimensions={1}, use_global_device_ids=true | all-gather | bytes 92160 | tf_op jit(solution)/shard_map/all_gather | solution.py:86
  128.0 3.5 %collective-permute-start = (bf16[1,192,2048]{2,1,0:T(8,128)(2,1)S(1)}, bf16[1,192,2048]{2,1,0:T(8,128)(2,1)S(1)}, u32[]{:S(2)}, u32[]{:S(2)}) collective-permute-start(bf16[1,192,2048]{2,1,0:T(8,128)(2,1)S(1)} %fusion.1), channel_id=1, source_target_pairs={{0,8},{8,16},{16,24},{1,9},{9,17},{17,25},{2,10},{10,18},{18,26},{... | collective-permute-start | bytes 2359304 | tf_op jit(solution)/shard_map/ppermute | solution.py:17
  131.5 14.1 %collective-permute-done = bf16[1,192,2048]{2,1,0:T(8,128)(2,1)S(1)} collective-permute-done((bf16[1,192,2048]{2,1,0:T(8,128)(2,1)S(1)}, bf16[1,192,2048]{2,1,0:T(8,128)(2,1)S(1)}, u32[]{:S(2)}, u32[]{:S(2)}) %collective-permute-start) | collective-permute-done | bytes 786464 | tf_op jit(solution)/shard_map/ppermute | solution.py:17
  145.7 1.8 %fusion.39 = bf16[1,96,2048]{2,1,0:T(8,128)(2,1)} fusion(bf16[96,2048]{1,0:T(8,128)(2,1)} %reduce-scatter.12.cloned.1.call-done), kind=kLoop, calls=%fused_computation.50 | loop fusion | flops 589824 | bytes 786432 | tf_op jit(solution)/shard_map/broadcast_in_dim | solution.py:124
  147.5 1.8 %fusion.40 = bf16[1,96,2048]{2,1,0:T(8,128)(2,1)} fusion(bf16[96,2048]{1,0:T(8,128)(2,1)} %reduce-scatter.14.cloned.1.call-done), kind=kLoop, calls=%fused_computation.51 | loop fusion | flops 589824 | bytes 786432 | tf_op jit(solution)/shard_map/broadcast_in_dim | solution.py:124
  149.3 0.9 copy.13
  150.2 0.9 copy.14
  (38 shorter events, 3.6 us)
Async XLA Ops:
  7.2 13.7 %copy-start = (bf16[1,192,2048]{2,1,0:T(8,128)(2,1)S(1)}, bf16[1,192,2048]{2,1,0:T(8,128)(2,1)}, u32[]{:S(2)}) copy-start(bf16[1,192,2048]{2,1,0:T(8,128)(2,1)} %param.12) | copy-start | bytes 2359300
  7.2 39.6 %reduce-scatter.10.cloned.1.call-start = ((), (), s32[]{:S(2)}) async-start(), calls=%async_computation.7 | async-start | bytes 122880 | tf_op jit(solution)/shard_map/reduce_scatter | solution.py:78
  8.0 15.2 %copy-start.7 = (s32[1,1,2]{2,1,0:T(1,128)S(1)}, s32[1,1,2]{2,1,0:T(1,128)}, u32[]{:S(2)}) copy-start(s32[1,1,2]{2,1,0:T(1,128)} %param.10) | copy-start | bytes 28
  8.0 17.1 %copy-start.4 = (bf16[1,1,192,2048]{3,2,1,0:T(8,128)(2,1)S(1)}, bf16[1,1,192,2048]{3,2,1,0:T(8,128)(2,1)}, u32[]{:S(2)}) copy-start(bf16[1,1,192,2048]{3,2,1,0:T(8,128)(2,1)} %param.9) | copy-start | bytes 2359300
  23.1 4.4 %copy-start.2 = (bf16[1,1,192,2048]{3,2,1,0:T(8,128)(2,1)S(1)}, bf16[1,1,192,2048]{3,2,1,0:T(8,128)(2,1)}, u32[]{:S(2)}) copy-start(bf16[1,1,192,2048]{3,2,1,0:T(8,128)(2,1)} %param.7) | copy-start | bytes 2359300
  23.1 51.1 %reduce-scatter.8.cloned.1.call-start = ((), (), s32[]{:S(2)}) async-start(), calls=%async_computation.6 | async-start | bytes 122880 | tf_op jit(solution)/shard_map/reduce_scatter | solution.py:81
  25.1 58.3 %copy-start.1 = (bf16[1,1,192,2048]{3,2,1,0:T(8,128)(2,1)S(1)}, bf16[1,1,192,2048]{3,2,1,0:T(8,128)(2,1)}, u32[]{:S(2)}) copy-start(bf16[1,1,192,2048]{3,2,1,0:T(8,128)(2,1)} %param.8) | copy-start | bytes 2359300
  27.5 91.0 %reduce-scatter.6.cloned.1.call-start = ((), (), s32[]{:S(2)}) async-start(), calls=%async_computation.5 | async-start | bytes 122880 | tf_op jit(solution)/shard_map/reduce_scatter | solution.py:75
  95.1 50.6 %reduce-scatter.12.cloned.1.call-start = ((), (), s32[]{:S(2)}) async-start(), calls=%async_computation.8 | async-start | bytes 1179648 | tf_op jit(solution)/shard_map/reduce_scatter | solution.py:114
  96.5 51.0 %reduce-scatter.14.cloned.1.call-start = ((), (), s32[]{:S(2)}) async-start(), calls=%async_computation.9 | async-start | bytes 1179648 | tf_op jit(solution)/shard_map/reduce_scatter | solution.py:117
  96.6 11.5 %copy-start.5 = (bf16[1,1,192,2048]{3,2,1,0:T(8,128)(2,1)S(1)}, bf16[1,1,192,2048]{3,2,1,0:T(8,128)(2,1)}, u32[]{:S(2)}) copy-start(bf16[1,1,192,2048]{3,2,1,0:T(8,128)(2,1)} %param.9) | copy-start | bytes 2359300
  99.2 28.4 %copy-start.3 = (bf16[1,1,192,2048]{3,2,1,0:T(8,128)(2,1)S(1)}, bf16[1,1,192,2048]{3,2,1,0:T(8,128)(2,1)}, u32[]{:S(2)}) copy-start(bf16[1,1,192,2048]{3,2,1,0:T(8,128)(2,1)} %param.7) | copy-start | bytes 2359300
  99.2 28.4 %copy-start.6 = (bf16[1,192,2048]{2,1,0:T(8,128)(2,1)S(1)}, bf16[1,192,2048]{2,1,0:T(8,128)(2,1)}, u32[]{:S(2)}) copy-start(bf16[1,192,2048]{2,1,0:T(8,128)(2,1)} %param.13) | copy-start | bytes 2359300
  99.2 32.3 %collective-permute-start.1 = (bf16[1,192,2048]{2,1,0:T(8,128)(2,1)}, bf16[1,192,2048]{2,1,0:T(8,128)(2,1)S(1)}, u32[]{:S(2)}, u32[]{:S(2)}) collective-permute-start(bf16[1,192,2048]{2,1,0:T(8,128)(2,1)} %fusion.22), channel_id=1, source_target_pairs={{8,0},{16,8},{24,16},{9,1},{17,9},{25,17},{10,2},{18,10},{26,18},{... | collective-permute-start | bytes 2359304 | tf_op jit(solution)/shard_map/ppermute | solution.py:19
  128.0 17.7 %collective-permute-start = (bf16[1,192,2048]{2,1,0:T(8,128)(2,1)S(1)}, bf16[1,192,2048]{2,1,0:T(8,128)(2,1)S(1)}, u32[]{:S(2)}, u32[]{:S(2)}) collective-permute-start(bf16[1,192,2048]{2,1,0:T(8,128)(2,1)S(1)} %fusion.1), channel_id=1, source_target_pairs={{0,8},{8,16},{16,24},{1,9},{9,17},{17,25},{2,10},{10,18},{18,26},{... | collective-permute-start | bytes 2359304 | tf_op jit(solution)/shard_map/ppermute | solution.py:17
Sparse Core Ops, SparseCore 0:
  23.3 23.4 reduce-scatter.9
  50.1 24.1 reduce-scatter.7
  95.2 23.2 reduce-scatter.5
  121.1 8.1 reduce-scatter.11
  131.4 9.2 reduce-scatter.13
where the time goes:
time: 158 us
  waiting for transfers between devices  69.8 us (44%)
  blocking collectives  44.4 us (28%)
  between operations  13.9 us (9%)
  other arithmetic  11.6 us (7%)
  matrix products  10.4 us (7%)
  starting transfers between devices  5.13 us (3%)
  local copies, waits for them, and re-layouts  2.39 us (2%)
    reduce_scatter x1, waiting for transfers between devices, shards(): lax.psum_scatter(slope_part.astype(jnp.bfloat16), 'tensor', scatter_dimen...  27.5 us
    psum x2, blocking collectives, shards(): lax.psum((jnp.sum(forward_values * forward_values, axis=1), jnp.sum(saved...  20.3 us
    reduce_scatter x1, waiting for transfers between devices, shards(): lax.psum_scatter(saved_part.astype(jnp.bfloat16), 'tensor', scatter_dimen...  19 us
    ppermute x1, waiting for transfers between devices, padded_2(): lax.ppermute(tail, axis, [(i, (i + 1) % count) for i in range(ends)])  14.1 us
    reduce_scatter x1, waiting for transfers between devices, shards(): lax.psum_scatter(forward_part.astype(jnp.bfloat16), 'tensor', scatter_dim...  9.06 us
    all_gather x1, blocking collectives, shards(): lax.all_gather(jax.nn.silu(forward_share).astype(jnp.bfloat16), 'tensor',...  8.36 us
    all_gather x1, blocking collectives, shards(): lax.all_gather((slope_share * silu_slope(saved_share)).astype(jnp.bfloat1...  8.3 us
    all_gather x1, blocking collectives, shards(): lax.all_gather(jax.nn.silu(saved_share).astype(jnp.bfloat16), 'tensor', a...  7.44 us
  transfers between devices with their start and end apart: 7, of which 4 were waited for; matrix products, arithmetic and copies ran while one was open for 8% of the time, Pallas kernels for 0%

commit v1 on v0

v1 whole, which is shorter than its diff:
```python
import functools

import jax
import jax.numpy as jnp
from jax import lax
from jax.experimental import pallas as pl
from jax.experimental.pallas import tpu as pltpu
from jax.sharding import PartitionSpec as P

EPSILON = 1e-05
LANES = 128
F32 = jnp.float32
BF16 = jnp.bfloat16


def contract_last(left_side, right_side):
    return lax.dot_general(
        left_side, right_side, (((1,), (1,)), ((), ())), preferred_element_type=F32
    )


def contract_rows(left_side, right_side):
    return lax.dot_general(
        left_side, right_side, (((0,), (0,)), ((), ())), preferred_element_type=F32
    )


def flip(index, bit):
    step = 1 << bit
    return index + step * (1 - 2 * ((index // step) % 2))


def split_two(value):
    high = value.astype(BF16).astype(F32)
    return high, value - high


def tick(sizes, fwd_hbm, sav_hbm, grad_hbm, len_ref, gain_ref, down_hbm, up_hbm,
         next_in, next_gr, grad_down, grad_up,
         fwd, sav, kept, down, up, scaled,
         acc_f, acc_b, send_f, recv_f, send_b, recv_b, out_f, out_b,
         part, part_recv, load_sem,
         f_send_sem, f_recv_sem, b_send_sem, b_recv_sem,
         sec_send_sem, sec_recv_sem, dp_send_sem, dp_recv_sem):
    n_sec, n_ten, n_dp, chunk = sizes
    rows, width = fwd.shape
    rank = down.shape[0]
    full_width = width * n_ten
    n_seq = len_ref.shape[1]
    bits = n_ten.bit_length() - 1
    half = rows // 2
    n_chunk = width // chunk
    share = rank // n_dp
    sec, ten, dp = lax.axis_index("section"), lax.axis_index("tensor"), lax.axis_index("dp")

    loads = [
        pltpu.make_async_copy(src, dst, load_sem.at[i])
        for i, (src, dst) in enumerate(
            ((fwd_hbm, fwd), (down_hbm, down), (sav_hbm, sav), (grad_hbm, kept), (up_hbm, up))
        )
    ]
    for load in loads:
        load.start()

    barrier = pltpu.get_barrier_semaphore()
    for bit in range(bits):
        pl.semaphore_signal(barrier, inc=1, device_id={"tensor": flip(ten, bit)})
    for k in range(1, n_dp):
        pl.semaphore_signal(barrier, inc=1, device_id={"dp": (dp + k) % n_dp})

    @pl.when(sec > 0)
    def _():
        pl.semaphore_signal(barrier, inc=1, device_id={"section": sec - 1})

    @pl.when(sec < n_sec - 1)
    def _():
        pl.semaphore_signal(barrier, inc=1, device_id={"section": sec + 1})

    columns = [slice(c * chunk, (c + 1) * chunk) for c in range(n_chunk)]

    loads[0].wait()
    loads[1].wait()
    total = jnp.zeros((rows, rank), F32)
    square_f = jnp.zeros((rows, 1), F32)
    for cols in columns:
        values = fwd[:, cols].astype(F32)
        square_f += jnp.sum(values * values, axis=1, keepdims=True)
        gained = (values * gain_ref[:, cols].astype(F32)).astype(BF16)
        total += contract_last(gained, down[:, cols])
    loads[2].wait()
    square_s = jnp.zeros((rows, 1), F32)
    for cols in columns:
        values = sav[:, cols].astype(F32)
        square_s += jnp.sum(values * values, axis=1, keepdims=True)
        scaled[:, cols] = (values * gain_ref[:, cols].astype(F32)).astype(BF16)
    wide = acc_f.shape[1]
    packed = jnp.concatenate([total, jnp.zeros((rows, wide - rank), F32)], axis=1)
    lane = lax.broadcasted_iota(jnp.int32, (rows, wide), 1)
    for i, piece in enumerate(split_two(square_f) + split_two(square_s)):
        packed = jnp.where(lane == rank + i, piece, packed)
    acc_f[...] = packed

    pl.semaphore_wait(barrier, bits + n_dp - 1 + jnp.where(sec > 0, 1, 0) + jnp.where(sec < n_sec - 1, 1, 0))

    def exchange(send, recv, send_sem, recv_sem, h, p):
        span = pl.ds(h * half, half)
        return pltpu.make_async_remote_copy(
            src_ref=send.at[p, span],
            dst_ref=recv.at[p, span],
            send_sem=send_sem.at[h, p],
            recv_sem=recv_sem.at[h, p],
            device_id={"tensor": flip(ten, (h + p) % bits)},
        )

    forms = ((acc_f, send_f, recv_f, f_send_sem, f_recv_sem), (acc_b, send_b, recv_b, b_send_sem, b_recv_sem))

    def begin(form, p):
        acc, send, recv, send_sem, recv_sem = form
        for h in range(2):
            span = pl.ds(h * half, half)
            send[p, span] = acc[span].astype(BF16)
            exchange(send, recv, send_sem, recv_sem, h, p).start()

    def finish(form, p):
        acc, send, recv, send_sem, recv_sem = form
        for h in range(2):
            span = pl.ds(h * half, half)
            exchange(send, recv, send_sem, recv_sem, h, p).wait()
            acc[span] = acc[span] + recv[p, span].astype(F32)

    if bits:
        begin(forms[0], 0)

    total_s = jnp.zeros((rows, rank), F32)
    for cols in columns:
        total_s += contract_last(scaled[:, cols], down[:, cols])
    loads[3].wait()
    loads[4].wait()
    position = lax.broadcasted_iota(jnp.int32, (rows, 1), 0)
    seq_rows = rows // n_seq
    limit = jnp.full((rows, 1), 0, jnp.int32)
    for i in range(n_seq):
        limit = jnp.where(position >= i * seq_rows, i * seq_rows + len_ref[0, i], limit)
    keep = position < limit
    total_g = jnp.zeros((rows, rank), F32)
    for cols in columns:
        held = jnp.where(keep, kept[:, cols].astype(F32), 0.0).astype(BF16)
        kept[:, cols] = held
        total_g += contract_last(held, up[:, cols])
    acc_b[...] = jnp.concatenate([total_g, total_s], axis=1)
    if bits:
        begin(forms[1], 0)
    for p in range(1, bits):
        for form in forms:
            finish(form, p - 1)
            begin(form, p)
    if bits:
        finish(forms[0], bits - 1)

    lane = lax.broadcasted_iota(jnp.int32, (rows, wide), 1)
    reduced = acc_f[...]
    square_f = jnp.sum(jnp.where((lane == rank) | (lane == rank + 1), reduced, 0.0), axis=1, keepdims=True)
    square_s = jnp.sum(jnp.where((lane == rank + 2) | (lane == rank + 3), reduced, 0.0), axis=1, keepdims=True)
    scale_f = lax.rsqrt(square_f / full_width + EPSILON)
    scale_s = lax.rsqrt(square_s / full_width + EPSILON)

    def shift(way, source, target, c):
        span = pl.ds(c * chunk, chunk)
        return pltpu.make_async_remote_copy(
            src_ref=source.at[:, span],
            dst_ref=target.at[:, span],
            send_sem=sec_send_sem.at[way, c],
            recv_sem=sec_recv_sem.at[way, c],
            device_id={"section": sec + 1 if way == 0 else sec - 1},
        )

    rank_f = reduced[:, :rank] * scale_f
    act_f = (rank_f * jax.nn.sigmoid(rank_f)).astype(BF16)

    @pl.when(sec < n_sec - 1)
    def _():
        for c, cols in enumerate(columns):
            grown = jnp.dot(act_f, up[:, cols], preferred_element_type=F32)
            out_f[:, cols] = (fwd[:, cols].astype(F32) + grown).astype(BF16)
            shift(0, out_f, next_in, c).start()

    if bits:
        finish(forms[1], bits - 1)
    slope = acc_b[:, :rank]
    rank_s = acc_b[:, rank:] * scale_s
    gate = jax.nn.sigmoid(rank_s)
    act_s = (rank_s * gate).astype(BF16)
    back = slope * (gate * (1.0 + rank_s * (1.0 - gate)))
    back_b = back.astype(BF16)
    tilt = jnp.sum(back_b.astype(F32) * rank_s, axis=1, keepdims=True) * (scale_s * scale_s / full_width)

    @pl.when(sec > 0)
    def _():
        for c, cols in enumerate(columns):
            normed = jnp.dot(back_b, down[:, cols], preferred_element_type=F32)
            out_b[:, cols] = (
                kept[:, cols].astype(F32)
                + scale_s * (gain_ref[:, cols].astype(F32) * normed)
                - sav[:, cols].astype(F32) * tilt
            ).astype(BF16)
            shift(1, out_b, next_gr, c).start()

    back_scaled = (back * scale_s).astype(BF16)

    def trade(i, k):
        target = (dp + k) % n_dp
        return pltpu.make_async_remote_copy(
            src_ref=part.at[i, pl.ds(pl.multiple_of(target * share, share), share)],
            dst_ref=part_recv.at[i, k - 1],
            send_sem=dp_send_sem.at[i, k - 1],
            recv_sem=dp_recv_sem.at[i, k - 1],
            device_id={"dp": target},
        )

    for i, (left_side, right_side) in enumerate(((back_scaled, scaled), (act_s, kept))):
        for cols in columns:
            part[i, :, cols] = contract_rows(left_side, right_side[:, cols]).astype(BF16)
        for k in range(1, n_dp):
            trade(i, k).start()
    mine = pl.ds(pl.multiple_of(dp * share, share), share)
    for i, out in enumerate((grad_down, grad_up)):
        for k in range(1, n_dp):
            trade(i, k).wait()
        for cols in columns:
            summed = part[i, mine, cols].astype(F32)
            for k in range(1, n_dp):
                summed += part_recv[i, k - 1, :, cols].astype(F32)
            out[:, cols] = (summed * (1.0 / n_dp)).astype(BF16)

    @pl.when(sec == 0)
    def _():
        next_in[...] = jnp.zeros_like(next_in)

    @pl.when(sec == n_sec - 1)
    def _():
        next_gr[...] = jnp.zeros_like(next_gr)

    for c in range(n_chunk):
        @pl.when(sec < n_sec - 1)
        def _():
            shift(0, out_f, next_in, c).wait_send()
            shift(1, out_b, next_gr, c).wait_recv()

        @pl.when(sec > 0)
        def _():
            shift(1, out_b, next_gr, c).wait_send()
            shift(0, out_f, next_in, c).wait_recv()


def solution(mesh):
    n_sec, n_ten, n_dp = (mesh.shape[name] for name in ("section", "tensor", "dp"))

    def shards(forward_rows, saved_rows, output_grad, lengths, norm_gain, down_map, up_map):
        rows, width = forward_rows.shape[2:]
        rank = down_map.shape[1]
        share = rank // n_dp
        bits = n_ten.bit_length() - 1
        chunk = min(width, 4 * LANES)
        n_chunk = width // chunk
        wide = -(-(rank + 4) // LANES) * LANES
        steps = max(bits, 1)
        vmem = pl.BlockSpec(memory_space=pltpu.VMEM)
        anywhere = pl.BlockSpec(memory_space=pl.ANY)
        flops = 7 * 2 * rows * rank * width
        dma = pltpu.SemaphoreType.DMA
        results = pl.pallas_call(
            functools.partial(tick, (n_sec, n_ten, n_dp, chunk)),
            out_shape=(
                jax.ShapeDtypeStruct((rows, width), BF16),
                jax.ShapeDtypeStruct((rows, width), BF16),
                jax.ShapeDtypeStruct((share, width), BF16),
                jax.ShapeDtypeStruct((share, width), BF16),
            ),
            in_specs=[anywhere, anywhere, anywhere, pl.BlockSpec(memory_space=pltpu.SMEM), vmem, anywhere, anywhere],
            out_specs=(vmem,) * 4,
            scratch_shapes=[
                pltpu.VMEM((rows, width), BF16),
                pltpu.VMEM((rows, width), BF16),
                pltpu.VMEM((rows, width), BF16),
                pltpu.VMEM((rank, width), BF16),
                pltpu.VMEM((rank, width), BF16),
                pltpu.VMEM((rows, width), BF16),
                pltpu.VMEM((rows, wide), F32),
                pltpu.VMEM((rows, 2 * rank), F32),
                pltpu.VMEM((steps, rows, wide), BF16),
                pltpu.VMEM((steps, rows, wide), BF16),
                pltpu.VMEM((steps, rows, 2 * rank), BF16),
                pltpu.VMEM((steps, rows, 2 * rank), BF16),
                pltpu.VMEM((rows, width), BF16),
                pltpu.VMEM((rows, width), BF16),
                pltpu.VMEM((2, rank, width), BF16),
                pltpu.VMEM((2, max(n_dp - 1, 1), share, width), BF16),
                dma((5,)),
                dma((2, steps)),
                dma((2, steps)),
                dma((2, steps)),
                dma((2, steps)),
                dma((2, n_chunk)),
                dma((2, n_chunk)),
                dma((2, max(n_dp - 1, 1))),
                dma((2, max(n_dp - 1, 1))),
            ],
            compiler_params=pltpu.CompilerParams(collective_id=0, has_side_effects=True),
            cost_estimate=pl.CostEstimate(
                flops=flops, bytes_accessed=16 * rows * width, transcendentals=4 * rows * rank
            ),
            name="tick",
        )(
            forward_rows[0, 0], saved_rows[0, 0], output_grad[0, 0], lengths[0], norm_gain, down_map[0], up_map[0]
        )
        next_inputs, next_grads, grad_down, grad_up = results
        return next_inputs[None, None], next_grads[None, None], grad_down[None], grad_up[None]

    row_spec = P("section", "dp", None, "tensor")
    map_spec = P("section", None, "tensor")
    part_spec = P("section", "dp", "tensor")
    return jax.shard_map(
        shards,
        mesh=mesh,
        in_specs=(row_spec, row_spec, row_spec, P("section", "dp"), P("section", "tensor"), map_spec, map_spec),
        out_specs=(row_spec, row_spec, part_spec, part_spec),
        check_vma=False,
    )
```

time: 158 us -> 40.1 us (0.25)
  waiting for transfers between devices: 69.8 us -> 0 us
  blocking collectives: 44.4 us -> 0 us
  Pallas kernels: 0 us -> 33.8 us
  between operations: 13.9 us -> 0.65 us
  other arithmetic: 11.6 us -> 0 us
  matrix products: 10.4 us -> 0 us
  starting transfers between devices: 5.13 us -> 0 us
  local copies, waits for them, and re-layouts: 2.39 us -> 5.28 us
    reduce_scatter x5 -> x0, waiting for transfers between devices: 55.6 us -> none  [the longest x1 27.5 us: shards(): lax.psum_scatter(slope_part.astype(jnp.bfloat16), 'tensor', scatter_dimen...]
    pallas_call x0 -> x1, Pallas kernels: none -> 33.8 us  [shards(): pl.pallas_call(functools.partial(tick, (n_sec, n_ten, n_dp, chunk)), out_...]
    all_gather x3 -> x0, blocking collectives: 24.1 us -> none  [the longest x1 8.36 us: shards(): lax.all_gather(jax.nn.silu(forward_share).astype(jnp.bfloat16), 'tensor',...]
    psum x2 -> x0, blocking collectives: 20.3 us -> none  [shards(): lax.psum((jnp.sum(forward_values * forward_values, axis=1), jnp.sum(saved...]
    ppermute x2 -> x0, waiting for transfers between devices: 14.1 us -> none  [the longest x1 14.1 us: padded_2(): lax.ppermute(tail, axis, [(i, (i + 1) % count) for i in range(ends)])]
    dot_general x7 -> x0, matrix products: 10.4 us -> none  [the longest x3 6.81 us: contract_last(): lax.dot_general(left_side, right_side, (((1,), (1,)), ((), ())), preferre...]
    ppermute x2 -> x0, starting transfers between devices: 4.92 us -> none  [the longest x1 3.51 us: padded_2(): lax.ppermute(tail, axis, [(i, (i + 1) % count) for i in range(ends)])]
    broadcast_in_dim x2 -> x0, other arithmetic: 3.62 us -> none  [the longest x1 1.81 us: shards(): grad_down[None]]
  transfers between devices with their start and end apart: 7 -> 0, of which waited for: 4 -> 0; matrix products, arithmetic and copies ran while one was open for 8% -> 0% of each run, Pallas kernels for 0% -> 0%
where the time goes in v1:
time: 40.1 us; the launch traced here: 39.8 us
  Pallas kernels  33.8 us (84%)
  local copies, waits for them, and re-layouts  5.28 us (13%)
  between operations  0.65 us (2%)
    pallas_call x1, Pallas kernels, shards(): pl.pallas_call(functools.partial(tick, (n_sec, n_ten, n_dp, chunk)), out_...  33.8 us
    unnamed x10, local copies, waits for them, and re-layouts  5.28 us

profile of v1, /device:TPU:0, one launch (start us, length us, event | category | flops | bytes accessed | tf_op | source)
XLA Modules:
  0.0 39.8 jit_solution(6850731719776605611)
XLA Ops:
  0.6 33.8 %tick.1 = (bf16[192,2048]{1,0:T(8,128)(2,1)}, bf16[192,2048]{1,0:T(8,128)(2,1)}, bf16[96,2048]{1,0:T(8,128)(2,1)}, bf16[96,2048]{1,0:T(8,128)(2,1)}) custom-call(bf16[192,2048]{1,0:T(8,128)(2,1)} %bitcast.12, bf16[192,2048]{1,0:T(8,128)(2,1)} %bitcast.13, bf16[192,2048]{1,0:T(8,128)(2,1)} %bitcast.14, s32[1,2]{1,0:T(1,128)} %bitcast.19, ...), custom_call_target="tpu_custom_call" | custom-call | flops 1056964608 | bytes 6291456 | tf_op jit(solution)/shard_map/tick/pallas_call | solution.py:271
  34.5 0.0 copy-start
  34.5 2.2 %copy.15 = bf16[1,1,192,2048]{3,2,1,0:T(8,128)(2,1)} copy(bf16[1,1,192,2048]{3,2,1,0:T(8,128)(2,1)} %bitcast.11) | data formatting | bytes 1572864
  36.7 0.0 copy-done
  36.7 0.0 copy-start.2
  36.7 0.9 %copy.16 = bf16[1,1,192,2048]{3,2,1,0:T(8,128)(2,1)} copy(bf16[1,1,192,2048]{3,2,1,0:T(8,128)(2,1)S(1)} %bitcast.10) | data formatting | bytes 1572864
  37.5 0.4 copy-done.2
  37.9 0.0 copy-start.1
  37.9 0.7 %copy.17 = bf16[1,96,2048]{2,1,0:T(8,128)(2,1)} copy(bf16[1,96,2048]{2,1,0:T(8,128)(2,1)S(1)} %bitcast.18) | data formatting | bytes 786432
  38.6 0.4 copy-done.1
  39.0 0.7 %copy.18 = bf16[1,96,2048]{2,1,0:T(8,128)(2,1)} copy(bf16[1,96,2048]{2,1,0:T(8,128)(2,1)S(1)} %bitcast.17) | data formatting | bytes 786432
Async XLA Ops:
  34.5 2.2 %copy-start = (bf16[192,2048]{1,0:T(8,128)(2,1)S(1)}, bf16[192,2048]{1,0:T(8,128)(2,1)}, u32[]{:S(2)}) copy-start(bf16[192,2048]{1,0:T(8,128)(2,1)} %get-tuple-element.9) | copy-start | bytes 2359300
  36.7 1.2 %copy-start.2 = (bf16[96,2048]{1,0:T(8,128)(2,1)S(1)}, bf16[96,2048]{1,0:T(8,128)(2,1)}, u32[]{:S(2)}) copy-start(bf16[96,2048]{1,0:T(8,128)(2,1)} %get-tuple-element.10) | copy-start | bytes 1179652
  37.9 1.1 %copy-start.1 = (bf16[96,2048]{1,0:T(8,128)(2,1)S(1)}, bf16[96,2048]{1,0:T(8,128)(2,1)}, u32[]{:S(2)}) copy-start(bf16[96,2048]{1,0:T(8,128)(2,1)} %get-tuple-element.11) | copy-start | bytes 1179652

commit v2 on v1

--- a/solution.py
+++ b/solution.py
@@ -252,6 +252,16 @@
             shift(0, out_f, next_in, c).wait_recv()
 
 
+def place(*refs):
+    count = len(refs) // 2
+    sems = refs[-1]
+    copies = [pltpu.make_async_copy(refs[i], refs[count + i], sems.at[i]) for i in range(count)]
+    for copy in copies:
+        copy.start()
+    for copy in copies:
+        copy.wait()
+
+
 def solution(mesh):
     n_sec, n_ten, n_dp = (mesh.shape[name] for name in ("section", "tensor", "dp"))
 
@@ -268,14 +278,10 @@
         anywhere = pl.BlockSpec(memory_space=pl.ANY)
         flops = 7 * 2 * rows * rank * width
         dma = pltpu.SemaphoreType.DMA
+        shapes = ((rows, width),) * 2 + ((share, width),) * 2
         results = pl.pallas_call(
             functools.partial(tick, (n_sec, n_ten, n_dp, chunk)),
-            out_shape=(
-                jax.ShapeDtypeStruct((rows, width), BF16),
-                jax.ShapeDtypeStruct((rows, width), BF16),
-                jax.ShapeDtypeStruct((share, width), BF16),
-                jax.ShapeDtypeStruct((share, width), BF16),
-            ),
+            out_shape=tuple(pltpu.VMEM(shape, BF16) for shape in shapes),
             in_specs=[anywhere, anywhere, anywhere, pl.BlockSpec(memory_space=pltpu.SMEM), vmem, anywhere, anywhere],
             out_specs=(vmem,) * 4,
             scratch_shapes=[
@@ -313,7 +319,14 @@
         )(
             forward_rows[0, 0], saved_rows[0, 0], output_grad[0, 0], lengths[0], norm_gain, down_map[0], up_map[0]
         )
-        next_inputs, next_grads, grad_down, grad_up = results
+        next_inputs, next_grads, grad_down, grad_up = pl.pallas_call(
+            place,
+            out_shape=tuple(jax.ShapeDtypeStruct(shape, BF16) for shape in shapes),
+            in_specs=[vmem] * 4,
+            out_specs=(anywhere,) * 4,
+            scratch_shapes=[dma((4,))],
+            name="place",
+        )(*[pltpu.with_memory_space_constraint(x, pltpu.VMEM) for x in results])
         return next_inputs[None, None], next_grads[None, None], grad_down[None], grad_up[None]
 
     row_spec = P("section", "dp", None, "tensor")

time: 40.1 us -> 34.7 us (0.87)
  local copies, waits for them, and re-layouts: 5.28 us -> 0 us
    unnamed x10 -> x0, local copies, waits for them, and re-layouts: 5.28 us -> none
    pallas_call x0 -> x1, Pallas kernels: none -> 1.43 us  [shards(): pl.pallas_call(place, out_shape=tuple((jax.ShapeDtypeStruct(shape, BF16)...]
    pallas_call x1, Pallas kernels: 33.8 us -> 32.4 us  [shards(): pl.pallas_call(functools.partial(tick, (n_sec, n_ten, n_dp, chunk)), out_...]
where the time goes in v2:
time: 34.7 us; the launch traced here: 34.5 us
  Pallas kernels  33.9 us (98%)
  between operations  0.64 us (2%)
    pallas_call x1, Pallas kernels, shards(): pl.pallas_call(functools.partial(tick, (n_sec, n_ten, n_dp, chunk)), out_...  32.4 us
    pallas_call x1, Pallas kernels, shards(): pl.pallas_call(place, out_shape=tuple((jax.ShapeDtypeStruct(shape, BF16)...  1.43 us

profile of v2, /device:TPU:0, one launch (start us, length us, event | category | flops | bytes accessed | tf_op | source)
XLA Modules:
  0.0 34.5 jit_solution(3152783776805254499)
XLA Ops:
  0.6 32.4 %tick.1 = (bf16[192,2048]{1,0:T(8,128)(2,1)S(1)}, bf16[192,2048]{1,0:T(8,128)(2,1)S(1)}, bf16[96,2048]{1,0:T(8,128)(2,1)S(1)}, bf16[96,2048]{1,0:T(8,128)(2,1)S(1)}) custom-call(bf16[192,2048]{1,0:T(8,128)(2,1)} %bitcast.10, bf16[192,2048]{1,0:T(8,128)(2,1)} %bitcast.11, bf16[192,2048]{1,0:T(8,128)(2,1)} %bitcast.12, s32[1,2]{1,0:T(1,128)} %bitcast.15, ...), custom_call_target="tpu_custom_call" | custom-call | flops 1056964608 | bytes 6291456 | tf_op jit(solution)/shard_map/tick/pallas_call | solution.py:282
  33.1 1.4 %place.1 = (bf16[192,2048]{1,0:T(8,128)(2,1)}, bf16[192,2048]{1,0:T(8,128)(2,1)}, bf16[96,2048]{1,0:T(8,128)(2,1)}, bf16[96,2048]{1,0:T(8,128)(2,1)}) custom-call(bf16[192,2048]{1,0:T(8,128)(2,1)S(1)} %get-tuple-element.12.refs_0_, bf16[192,2048]{1,0:T(8,128)(2,1)S(1)} %get-tuple-element.13.refs_1_, bf16[96,2048]{1,0:T(8,128)(2,1)S(1)} %get-tuple-element.14.refs_2_, ...), custom_call_target="tpu_custom_call" | custom-call | tf_op jit(solution)/shard_map/place/pallas_call | solution.py:322

commit v3 on v2

--- a/solution.py
+++ b/solution.py
@@ -9,6 +9,8 @@
 
 EPSILON = 1e-05
 LANES = 128
+RAW_FORWARD = 0.375
+RAW_BACK = 0.25
 F32 = jnp.float32
 BF16 = jnp.bfloat16
 
@@ -39,9 +41,11 @@
          next_in, next_gr, grad_down, grad_up,
          fwd, sav, kept, down, up, scaled,
          acc_f, acc_b, send_f, recv_f, send_b, recv_b, out_f, out_b,
-         part, part_recv, load_sem,
+         part, part_recv, act_out, act_in, back_out, back_in,
+         raw_fwd, raw_up, raw_sav, raw_grad, raw_down, raw_gain, load_sem,
          f_send_sem, f_recv_sem, b_send_sem, b_recv_sem,
-         sec_send_sem, sec_recv_sem, dp_send_sem, dp_recv_sem):
+         sec_send_sem, sec_recv_sem, dp_send_sem, dp_recv_sem,
+         raw_send_sem, raw_recv_sem, relay_send_sem, relay_recv_sem):
     n_sec, n_ten, n_dp, chunk = sizes
     rows, width = fwd.shape
     rank = down.shape[0]
@@ -77,6 +81,50 @@
         pl.semaphore_signal(barrier, inc=1, device_id={"section": sec + 1})
 
     columns = [slice(c * chunk, (c + 1) * chunk) for c in range(n_chunk)]
+    raw_f, raw_b = raw_fwd.shape[1], raw_sav.shape[1]
+    mine = pl.ds(pl.multiple_of(dp * share, share), share)
+    tail_f, tail_b = pl.ds(width - raw_f, raw_f), pl.ds(width - raw_b, raw_b)
+
+    def across(i, source, target, step):
+        return pltpu.make_async_remote_copy(
+            src_ref=source,
+            dst_ref=target,
+            send_sem=raw_send_sem.at[i],
+            recv_sem=raw_recv_sem.at[i],
+            device_id={"section": sec + step},
+        )
+
+    raw_ups = across(0, up_hbm.at[mine, tail_f], raw_up.at[mine], 1)
+    raw_fwds = across(1, fwd_hbm.at[:, tail_f], raw_fwd, 1)
+    acts = across(2, act_out, act_in, 1)
+    raw_downs = across(3, down_hbm.at[mine, tail_b], raw_down.at[mine], -1)
+    raw_gains = across(4, gain_ref, raw_gain, -1)
+    raw_savs = across(5, sav_hbm.at[:, tail_b], raw_sav, -1)
+    raw_grads = across(6, grad_hbm.at[:, tail_b], raw_grad, -1)
+    backs = across(7, back_out, back_in, -1)
+    up_way, down_way = (raw_ups, raw_fwds, acts), (raw_downs, raw_gains, raw_savs, raw_grads, backs)
+
+    def relay(way, k):
+        ref = (raw_up, raw_down)[way].at[mine]
+        return pltpu.make_async_remote_copy(
+            src_ref=ref,
+            dst_ref=ref,
+            send_sem=relay_send_sem.at[way, k - 1],
+            recv_sem=relay_recv_sem.at[way, k - 1],
+            device_id={"dp": (dp + k) % n_dp},
+        )
+
+    pl.semaphore_wait(barrier, bits + n_dp - 1 + jnp.where(sec > 0, 1, 0) + jnp.where(sec < n_sec - 1, 1, 0))
+
+    @pl.when(sec < n_sec - 1)
+    def _():
+        for copy in up_way[:-1]:
+            copy.start()
+
+    @pl.when(sec > 0)
+    def _():
+        for copy in down_way[:-1]:
+            copy.start()
 
     loads[0].wait()
     loads[1].wait()
@@ -99,8 +147,6 @@
     for i, piece in enumerate(split_two(square_f) + split_two(square_s)):
         packed = jnp.where(lane == rank + i, piece, packed)
     acc_f[...] = packed
-
-    pl.semaphore_wait(barrier, bits + n_dp - 1 + jnp.where(sec > 0, 1, 0) + jnp.where(sec < n_sec - 1, 1, 0))
 
     def exchange(send, recv, send_sem, recv_sem, h, p):
         span = pl.ds(h * half, half)
@@ -164,8 +210,12 @@
     scale_f = lax.rsqrt(square_f / full_width + EPSILON)
     scale_s = lax.rsqrt(square_s / full_width + EPSILON)
 
+    done_f = [slice(a, min(a + chunk, width - raw_f)) for a in range(0, width - raw_f, chunk)]
+    done_b = [slice(a, min(a + chunk, width - raw_b)) for a in range(0, width - raw_b, chunk)]
+
     def shift(way, source, target, c):
-        span = pl.ds(c * chunk, chunk)
+        cols = (done_f, done_b)[way][c]
+        span = pl.ds(cols.start, cols.stop - cols.start)
         return pltpu.make_async_remote_copy(
             src_ref=source.at[:, span],
             dst_ref=target.at[:, span],
@@ -175,11 +225,18 @@
         )
 
     rank_f = reduced[:, :rank] * scale_f
-    act_f = (rank_f * jax.nn.sigmoid(rank_f)).astype(BF16)
-
-    @pl.when(sec < n_sec - 1)
-    def _():
-        for c, cols in enumerate(columns):
+    act_f = rank_f * jax.nn.sigmoid(rank_f)
+
+    @pl.when(sec < n_sec - 1)
+    def _():
+        act_out[...] = jnp.concatenate([act_f[:half], act_f[half:]], axis=1).astype(BF16)
+        acts.start()
+
+    act_f = act_f.astype(BF16)
+
+    @pl.when(sec < n_sec - 1)
+    def _():
+        for c, cols in enumerate(done_f):
             grown = jnp.dot(act_f, up[:, cols], preferred_element_type=F32)
             out_f[:, cols] = (fwd[:, cols].astype(F32) + grown).astype(BF16)
             shift(0, out_f, next_in, c).start()
@@ -194,18 +251,24 @@
     back_b = back.astype(BF16)
     tilt = jnp.sum(back_b.astype(F32) * rank_s, axis=1, keepdims=True) * (scale_s * scale_s / full_width)
 
-    @pl.when(sec > 0)
-    def _():
-        for c, cols in enumerate(columns):
-            normed = jnp.dot(back_b, down[:, cols], preferred_element_type=F32)
+    back_s = back * scale_s
+    back_scaled = back_s.astype(BF16)
+
+    @pl.when(sec > 0)
+    def _():
+        message = jnp.concatenate([back_s, jnp.zeros((rows, wide - rank), F32)], axis=1)
+        for i, piece in enumerate(split_two(tilt) + (jnp.where(keep, 1.0, 0.0),)):
+            message = jnp.where(lane == rank + i, piece, message)
+        back_out[...] = message.astype(BF16)
+        backs.start()
+        for c, cols in enumerate(done_b):
+            normed = jnp.dot(back_scaled, down[:, cols], preferred_element_type=F32)
             out_b[:, cols] = (
                 kept[:, cols].astype(F32)
-                + scale_s * (gain_ref[:, cols].astype(F32) * normed)
+                + gain_ref[:, cols].astype(F32) * normed
                 - sav[:, cols].astype(F32) * tilt
             ).astype(BF16)
             shift(1, out_b, next_gr, c).start()
-
-    back_scaled = (back * scale_s).astype(BF16)
 
     def trade(i, k):
         target = (dp + k) % n_dp
@@ -222,7 +285,19 @@
             part[i, :, cols] = contract_rows(left_side, right_side[:, cols]).astype(BF16)
         for k in range(1, n_dp):
             trade(i, k).start()
-    mine = pl.ds(pl.multiple_of(dp * share, share), share)
+
+    @pl.when(sec > 0)
+    def _():
+        raw_ups.wait_recv()
+        for k in range(1, n_dp):
+            relay(0, k).start()
+
+    @pl.when(sec < n_sec - 1)
+    def _():
+        raw_downs.wait_recv()
+        for k in range(1, n_dp):
+            relay(1, k).start()
+
     for i, out in enumerate((grad_down, grad_up)):
         for k in range(1, n_dp):
             trade(i, k).wait()
@@ -240,15 +315,57 @@
     def _():
         next_gr[...] = jnp.zeros_like(next_gr)
 
-    for c in range(n_chunk):
-        @pl.when(sec < n_sec - 1)
-        def _():
+    @pl.when(sec > 0)
+    def _():
+        for k in range(1, n_dp):
+            relay(0, k).wait()
+        raw_fwds.wait_recv()
+        acts.wait_recv()
+        came = act_in[...].astype(F32)
+        came = jnp.concatenate([came[:, :rank], came[:, rank:]], axis=0).astype(BF16)
+        for a in range(0, raw_f, chunk):
+            b = min(a + chunk, raw_f)
+            grown = jnp.dot(came, raw_up[:, a:b], preferred_element_type=F32)
+            next_in[:, width - raw_f + a:width - raw_f + b] = (raw_fwd[:, a:b].astype(F32) + grown).astype(BF16)
+
+    @pl.when(sec < n_sec - 1)
+    def _():
+        for k in range(1, n_dp):
+            relay(1, k).wait()
+        raw_gains.wait_recv()
+        raw_savs.wait_recv()
+        raw_grads.wait_recv()
+        backs.wait_recv()
+        came = back_in[...].astype(F32)
+        far_tilt = jnp.sum(jnp.where((lane == rank) | (lane == rank + 1), came, 0.0), axis=1, keepdims=True)
+        far_keep = jnp.sum(jnp.where(lane == rank + 2, came, 0.0), axis=1, keepdims=True)
+        far_back = came[:, :rank].astype(BF16)
+        for a in range(0, raw_b, chunk):
+            b = min(a + chunk, raw_b)
+            cols = slice(width - raw_b + a, width - raw_b + b)
+            normed = jnp.dot(far_back, raw_down[:, a:b], preferred_element_type=F32)
+            next_gr[:, cols] = (
+                jnp.where(far_keep > 0.5, raw_grad[:, a:b].astype(F32), 0.0)
+                + raw_gain[:, cols].astype(F32) * normed
+                - raw_sav[:, a:b].astype(F32) * far_tilt
+            ).astype(BF16)
+
+    @pl.when(sec < n_sec - 1)
+    def _():
+        for copy in up_way:
+            copy.wait_send()
+        for c in range(len(done_f)):
             shift(0, out_f, next_in, c).wait_send()
+        for c in range(len(done_b)):
             shift(1, out_b, next_gr, c).wait_recv()
 
-        @pl.when(sec > 0)
-        def _():
+    @pl.when(sec > 0)
+    def _():
+        for copy in down_way:
+            copy.wait_send()
+        for c in range(len(done_b)):
             shift(1, out_b, next_gr, c).wait_send()
+        for c in range(len(done_f)):
             shift(0, out_f, next_in, c).wait_recv()
 
 
@@ -272,6 +389,8 @@
         bits = n_ten.bit_length() - 1
         chunk = min(width, 4 * LANES)
         n_chunk = width // chunk
+        raw_f = int(width * RAW_FORWARD) // LANES * LANES
+        raw_b = int(width * RAW_BACK) // LANES * LANES
         wide = -(-(rank + 4) // LANES) * LANES
         steps = max(bits, 1)
         vmem = pl.BlockSpec(memory_space=pltpu.VMEM)
@@ -301,6 +420,16 @@
                 pltpu.VMEM((rows, width), BF16),
                 pltpu.VMEM((2, rank, width), BF16),
                 pltpu.VMEM((2, max(n_dp - 1, 1), share, width), BF16),
+                pltpu.VMEM((rows // 2, 2 * rank), BF16),
+                pltpu.VMEM((rows // 2, 2 * rank), BF16),
+                pltpu.VMEM((rows, wide), BF16),
+                pltpu.VMEM((rows, wide), BF16),
+                pltpu.VMEM((rows, raw_f), BF16),
+                pltpu.VMEM((rank, raw_f), BF16),
+                pltpu.VMEM((rows, raw_b), BF16),
+                pltpu.VMEM((rows, raw_b), BF16),
+                pltpu.VMEM((rank, raw_b), BF16),
+                pltpu.VMEM((1, width), BF16),
                 dma((5,)),
                 dma((2, steps)),
                 dma((2, steps)),
@@ -308,6 +437,10 @@
                 dma((2, steps)),
                 dma((2, n_chunk)),
                 dma((2, n_chunk)),
+                dma((2, max(n_dp - 1, 1))),
+                dma((2, max(n_dp - 1, 1))),
+                dma((8,)),
+                dma((8,)),
                 dma((2, max(n_dp - 1, 1))),
                 dma((2, max(n_dp - 1, 1))),
             ],

time: 34.7 us -> 34.3 us (0.988)
  Pallas kernels: 33.9 us -> 33.4 us
    pallas_call x1, Pallas kernels: 32.4 us -> 32 us  [shards(): pl.pallas_call(functools.partial(tick, (n_sec, n_ten, n_dp, chunk)), out_...]
where the time goes in v3:
time: 34.3 us; the launch traced here: 34.1 us
  Pallas kernels  33.4 us (97%)
  between operations  0.64 us (2%)
    pallas_call x1, Pallas kernels, shards(): pl.pallas_call(functools.partial(tick, (n_sec, n_ten, n_dp, chunk)), out_...  32 us
    pallas_call x1, Pallas kernels, shards(): pl.pallas_call(place, out_shape=tuple((jax.ShapeDtypeStruct(shape, BF16)...  1.43 us

profile of v3, /device:TPU:0, one launch (start us, length us, event | category | flops | bytes accessed | tf_op | source)
XLA Modules:
  0.0 34.1 jit_solution(14007736436263219512)
XLA Ops:
  0.6 32.0 %tick.1 = (bf16[192,2048]{1,0:T(8,128)(2,1)S(1)}, bf16[192,2048]{1,0:T(8,128)(2,1)S(1)}, bf16[96,2048]{1,0:T(8,128)(2,1)S(1)}, bf16[96,2048]{1,0:T(8,128)(2,1)S(1)}) custom-call(bf16[192,2048]{1,0:T(8,128)(2,1)} %bitcast.10, bf16[192,2048]{1,0:T(8,128)(2,1)} %bitcast.11, bf16[192,2048]{1,0:T(8,128)(2,1)} %bitcast.12, s32[1,2]{1,0:T(1,128)} %bitcast.15, ...), custom_call_target="tpu_custom_call" | custom-call | flops 1056964608 | bytes 6291456 | tf_op jit(solution)/shard_map/tick/pallas_call | solution.py:401
  32.6 1.4 %place.1 = (bf16[192,2048]{1,0:T(8,128)(2,1)}, bf16[192,2048]{1,0:T(8,128)(2,1)}, bf16[96,2048]{1,0:T(8,128)(2,1)}, bf16[96,2048]{1,0:T(8,128)(2,1)}) custom-call(bf16[192,2048]{1,0:T(8,128)(2,1)S(1)} %get-tuple-element.12.refs_0_, bf16[192,2048]{1,0:T(8,128)(2,1)S(1)} %get-tuple-element.13.refs_1_, bf16[96,2048]{1,0:T(8,128)(2,1)S(1)} %get-tuple-element.14.refs_2_, ...), custom_call_target="tpu_custom_call" | custom-call | tf_op jit(solution)/shard_map/place/pallas_call | solution.py:455

commit v4 on v3

--- a/solution.py
+++ b/solution.py
@@ -10,7 +10,8 @@
 EPSILON = 1e-05
 LANES = 128
 RAW_FORWARD = 0.375
-RAW_BACK = 0.25
+RAW_BACK = 0.125
+BLOCKS = 4
 F32 = jnp.float32
 BF16 = jnp.bfloat16
 
@@ -30,11 +31,6 @@
 def flip(index, bit):
     step = 1 << bit
     return index + step * (1 - 2 * ((index // step) % 2))
-
-
-def split_two(value):
-    high = value.astype(BF16).astype(F32)
-    return high, value - high
 
 
 def tick(sizes, fwd_hbm, sav_hbm, grad_hbm, len_ref, gain_ref, down_hbm, up_hbm,
@@ -42,6 +38,7 @@
          fwd, sav, kept, down, up, scaled,
          acc_f, acc_b, send_f, recv_f, send_b, recv_b, out_f, out_b,
          part, part_recv, act_out, act_in, back_out, back_in,
+         side_out, side_in, sq_out, sq_in, sq_send_sem, sq_recv_sem,
          raw_fwd, raw_up, raw_sav, raw_grad, raw_down, raw_gain, load_sem,
          f_send_sem, f_recv_sem, b_send_sem, b_recv_sem,
          sec_send_sem, sec_recv_sem, dp_send_sem, dp_recv_sem,
@@ -63,12 +60,12 @@
             ((fwd_hbm, fwd), (down_hbm, down), (sav_hbm, sav), (grad_hbm, kept), (up_hbm, up))
         )
     ]
-    for load in loads:
-        load.start()
+    for i in (2, 1, 3, 4, 0):
+        loads[i].start()
 
     barrier = pltpu.get_barrier_semaphore()
-    for bit in range(bits):
-        pl.semaphore_signal(barrier, inc=1, device_id={"tensor": flip(ten, bit)})
+    for k in range(1, n_ten):
+        pl.semaphore_signal(barrier, inc=1, device_id={"tensor": (ten + k) % n_ten})
     for k in range(1, n_dp):
         pl.semaphore_signal(barrier, inc=1, device_id={"dp": (dp + k) % n_dp})
 
@@ -102,7 +99,8 @@
     raw_savs = across(5, sav_hbm.at[:, tail_b], raw_sav, -1)
     raw_grads = across(6, grad_hbm.at[:, tail_b], raw_grad, -1)
     backs = across(7, back_out, back_in, -1)
-    up_way, down_way = (raw_ups, raw_fwds, acts), (raw_downs, raw_gains, raw_savs, raw_grads, backs)
+    sides = across(8, side_out, side_in, -1)
+    up_way, down_way = (raw_ups, raw_fwds, acts), (raw_downs, raw_gains, raw_savs, raw_grads, backs, sides)
 
     def relay(way, k):
         ref = (raw_up, raw_down)[way].at[mine]
@@ -114,7 +112,7 @@
             device_id={"dp": (dp + k) % n_dp},
         )
 
-    pl.semaphore_wait(barrier, bits + n_dp - 1 + jnp.where(sec > 0, 1, 0) + jnp.where(sec < n_sec - 1, 1, 0))
+    pl.semaphore_wait(barrier, n_ten - 1 + n_dp - 1 + jnp.where(sec > 0, 1, 0) + jnp.where(sec < n_sec - 1, 1, 0))
 
     @pl.when(sec < n_sec - 1)
     def _():
@@ -123,65 +121,78 @@
 
     @pl.when(sec > 0)
     def _():
-        for copy in down_way[:-1]:
+        for copy in down_way[:-2]:
             copy.start()
 
-    loads[0].wait()
-    loads[1].wait()
-    total = jnp.zeros((rows, rank), F32)
-    square_f = jnp.zeros((rows, 1), F32)
-    for cols in columns:
-        values = fwd[:, cols].astype(F32)
-        square_f += jnp.sum(values * values, axis=1, keepdims=True)
-        gained = (values * gain_ref[:, cols].astype(F32)).astype(BF16)
-        total += contract_last(gained, down[:, cols])
-    loads[2].wait()
+    def exchange(form, q, p):
+        acc, send, recv, send_sem, recv_sem, blocks = form
+        span = pl.ds(q * (rows // blocks), rows // blocks)
+        return pltpu.make_async_remote_copy(
+            src_ref=send.at[p, span],
+            dst_ref=recv.at[p, span],
+            send_sem=send_sem.at[q, p],
+            recv_sem=recv_sem.at[q, p],
+            device_id={"tensor": flip(ten, (q + p) % bits)},
+        )
+
+    form_f = (acc_f, send_f, recv_f, f_send_sem, f_recv_sem, 2)
+    form_b = (acc_b, send_b, recv_b, b_send_sem, b_recv_sem, BLOCKS)
+
+    def begin(form, q, p):
+        acc, send, blocks = form[0], form[1], form[5]
+        span = pl.ds(q * (rows // blocks), rows // blocks)
+        send[p, span] = acc[span].astype(BF16)
+        exchange(form, q, p).start()
+
+    def finish(form, q, p):
+        acc, recv, blocks = form[0], form[2], form[5]
+        span = pl.ds(q * (rows // blocks), rows // blocks)
+        exchange(form, q, p).wait()
+        acc[span] = acc[span] + recv[p, span].astype(F32)
+
+    eye = lax.broadcasted_iota(jnp.int32, (rows, rows), 0) == lax.broadcasted_iota(jnp.int32, (rows, rows), 1)
+
+    def to_row(column):
+        return jnp.sum(jnp.where(eye, column, 0.0), axis=0, keepdims=True)
+
+    def to_column(row):
+        return jnp.sum(jnp.where(eye, row, 0.0), axis=1, keepdims=True)
+
+    def squares(i, k):
+        return pltpu.make_async_remote_copy(
+            src_ref=sq_out.at[i],
+            dst_ref=sq_in.at[i, k - 1],
+            send_sem=sq_send_sem.at[i, k - 1],
+            recv_sem=sq_recv_sem.at[i, k - 1],
+            device_id={"tensor": (ten + k) % n_ten},
+        )
+
+    def spread(i, column):
+        sq_out[i] = jnp.broadcast_to(to_row(column), (8, rows))
+        for k in range(1, n_ten):
+            squares(i, k).start()
+
+    def scale_of(i):
+        row = sq_out[i, 0:1]
+        for k in range(1, n_ten):
+            squares(i, k).wait()
+            row += sq_in[i, k - 1, 0:1]
+        return lax.rsqrt(to_column(row) / full_width + EPSILON)
+
+    load_fwd, load_down, load_sav, load_grad, load_up = loads
+    load_sav.wait()
     square_s = jnp.zeros((rows, 1), F32)
     for cols in columns:
         values = sav[:, cols].astype(F32)
         square_s += jnp.sum(values * values, axis=1, keepdims=True)
         scaled[:, cols] = (values * gain_ref[:, cols].astype(F32)).astype(BF16)
-    wide = acc_f.shape[1]
-    packed = jnp.concatenate([total, jnp.zeros((rows, wide - rank), F32)], axis=1)
-    lane = lax.broadcasted_iota(jnp.int32, (rows, wide), 1)
-    for i, piece in enumerate(split_two(square_f) + split_two(square_s)):
-        packed = jnp.where(lane == rank + i, piece, packed)
-    acc_f[...] = packed
-
-    def exchange(send, recv, send_sem, recv_sem, h, p):
-        span = pl.ds(h * half, half)
-        return pltpu.make_async_remote_copy(
-            src_ref=send.at[p, span],
-            dst_ref=recv.at[p, span],
-            send_sem=send_sem.at[h, p],
-            recv_sem=recv_sem.at[h, p],
-            device_id={"tensor": flip(ten, (h + p) % bits)},
-        )
-
-    forms = ((acc_f, send_f, recv_f, f_send_sem, f_recv_sem), (acc_b, send_b, recv_b, b_send_sem, b_recv_sem))
-
-    def begin(form, p):
-        acc, send, recv, send_sem, recv_sem = form
-        for h in range(2):
-            span = pl.ds(h * half, half)
-            send[p, span] = acc[span].astype(BF16)
-            exchange(send, recv, send_sem, recv_sem, h, p).start()
-
-    def finish(form, p):
-        acc, send, recv, send_sem, recv_sem = form
-        for h in range(2):
-            span = pl.ds(h * half, half)
-            exchange(send, recv, send_sem, recv_sem, h, p).wait()
-            acc[span] = acc[span] + recv[p, span].astype(F32)
-
-    if bits:
-        begin(forms[0], 0)
-
+    spread(0, square_s)
+    load_down.wait()
     total_s = jnp.zeros((rows, rank), F32)
     for cols in columns:
         total_s += contract_last(scaled[:, cols], down[:, cols])
-    loads[3].wait()
-    loads[4].wait()
+    load_grad.wait()
+    load_up.wait()
     position = lax.broadcasted_iota(jnp.int32, (rows, 1), 0)
     seq_rows = rows // n_seq
     limit = jnp.full((rows, 1), 0, jnp.int32)
@@ -195,36 +206,95 @@
         total_g += contract_last(held, up[:, cols])
     acc_b[...] = jnp.concatenate([total_g, total_s], axis=1)
     if bits:
-        begin(forms[1], 0)
+        for q in range(BLOCKS):
+            begin(form_b, q, 0)
+
+    load_fwd.wait()
+    total = jnp.zeros((rows, rank), F32)
+    square_f = jnp.zeros((rows, 1), F32)
+    for cols in columns:
+        values = fwd[:, cols].astype(F32)
+        square_f += jnp.sum(values * values, axis=1, keepdims=True)
+        gained = (values * gain_ref[:, cols].astype(F32)).astype(BF16)
+        total += contract_last(gained, down[:, cols])
+    acc_f[...] = total
+    spread(1, square_f)
+    if bits:
+        for q in range(2):
+            begin(form_f, q, 0)
     for p in range(1, bits):
-        for form in forms:
-            finish(form, p - 1)
-            begin(form, p)
-    if bits:
-        finish(forms[0], bits - 1)
-
-    lane = lax.broadcasted_iota(jnp.int32, (rows, wide), 1)
-    reduced = acc_f[...]
-    square_f = jnp.sum(jnp.where((lane == rank) | (lane == rank + 1), reduced, 0.0), axis=1, keepdims=True)
-    square_s = jnp.sum(jnp.where((lane == rank + 2) | (lane == rank + 3), reduced, 0.0), axis=1, keepdims=True)
-    scale_f = lax.rsqrt(square_f / full_width + EPSILON)
-    scale_s = lax.rsqrt(square_s / full_width + EPSILON)
+        for q in range(BLOCKS):
+            finish(form_b, q, p - 1)
+            begin(form_b, q, p)
+        for q in range(2):
+            finish(form_f, q, p - 1)
+            begin(form_f, q, p)
 
     done_f = [slice(a, min(a + chunk, width - raw_f)) for a in range(0, width - raw_f, chunk)]
     done_b = [slice(a, min(a + chunk, width - raw_b)) for a in range(0, width - raw_b, chunk)]
 
-    def shift(way, source, target, c):
+    def shift(way, source, target, g, c):
         cols = (done_f, done_b)[way][c]
         span = pl.ds(cols.start, cols.stop - cols.start)
+        part_rows = pl.ds(g * half, half)
         return pltpu.make_async_remote_copy(
-            src_ref=source.at[:, span],
-            dst_ref=target.at[:, span],
-            send_sem=sec_send_sem.at[way, c],
-            recv_sem=sec_recv_sem.at[way, c],
+            src_ref=source.at[part_rows, span],
+            dst_ref=target.at[part_rows, span],
+            send_sem=sec_send_sem.at[way, g, c],
+            recv_sem=sec_recv_sem.at[way, g, c],
             device_id={"section": sec + 1 if way == 0 else sec - 1},
         )
 
-    rank_f = reduced[:, :rank] * scale_f
+    def shifts(way):
+        source, target = ((out_f, next_in), (out_b, next_gr))[way]
+        return [shift(way, source, target, g, c) for g in range(2) for c in range(len((done_f, done_b)[way]))]
+
+    scale_s = scale_of(0)
+    acts_s, backs_s, tilts = [], [], []
+    for g in range(2):
+        span = slice(g * half, (g + 1) * half)
+        if bits:
+            for q in range(g * BLOCKS // 2, (g + 1) * BLOCKS // 2):
+                finish(form_b, q, bits - 1)
+        own_scale = scale_s[span]
+        slope = acc_b[span, :rank]
+        rank_s = acc_b[span, rank:] * own_scale
+        gate = jax.nn.sigmoid(rank_s)
+        acts_s.append((rank_s * gate).astype(BF16))
+        back = slope * (gate * (1.0 + rank_s * (1.0 - gate)))
+        tilt = jnp.sum(back.astype(BF16).astype(F32) * rank_s, axis=1, keepdims=True) * (own_scale * own_scale / full_width)
+        back_s = back * own_scale
+        back_rows = back_s.astype(BF16)
+        backs_s.append(back_s)
+        tilts.append(tilt)
+
+        @pl.when(sec > 0)
+        def _():
+            if g == 1:
+                back_out[...] = jnp.concatenate(backs_s, axis=1).astype(BF16)
+                top = lax.broadcasted_iota(jnp.int32, (8, rows), 0) == 0
+                side_out[...] = jnp.where(
+                    top, to_row(jnp.concatenate(tilts, axis=0)), to_row(jnp.where(keep, 1.0, 0.0))
+                )
+                backs.start()
+                sides.start()
+            for c, cols in enumerate(done_b):
+                normed = jnp.dot(back_rows, down[:, cols], preferred_element_type=F32)
+                out_b[span, cols] = (
+                    kept[span, cols].astype(F32)
+                    + gain_ref[:, cols].astype(F32) * normed
+                    - sav[span, cols].astype(F32) * tilt
+                ).astype(BF16)
+                shift(1, out_b, next_gr, g, c).start()
+
+    back_scaled = jnp.concatenate(backs_s, axis=0).astype(BF16)
+    act_s = jnp.concatenate(acts_s, axis=0)
+
+    scale_f = scale_of(1)
+    if bits:
+        for q in range(2):
+            finish(form_f, q, bits - 1)
+    rank_f = acc_f[...] * scale_f
     act_f = rank_f * jax.nn.sigmoid(rank_f)
 
     @pl.when(sec < n_sec - 1)
@@ -239,36 +309,8 @@
         for c, cols in enumerate(done_f):
             grown = jnp.dot(act_f, up[:, cols], preferred_element_type=F32)
             out_f[:, cols] = (fwd[:, cols].astype(F32) + grown).astype(BF16)
-            shift(0, out_f, next_in, c).start()
-
-    if bits:
-        finish(forms[1], bits - 1)
-    slope = acc_b[:, :rank]
-    rank_s = acc_b[:, rank:] * scale_s
-    gate = jax.nn.sigmoid(rank_s)
-    act_s = (rank_s * gate).astype(BF16)
-    back = slope * (gate * (1.0 + rank_s * (1.0 - gate)))
-    back_b = back.astype(BF16)
-    tilt = jnp.sum(back_b.astype(F32) * rank_s, axis=1, keepdims=True) * (scale_s * scale_s / full_width)
-
-    back_s = back * scale_s
-    back_scaled = back_s.astype(BF16)
-
-    @pl.when(sec > 0)
-    def _():
-        message = jnp.concatenate([back_s, jnp.zeros((rows, wide - rank), F32)], axis=1)
-        for i, piece in enumerate(split_two(tilt) + (jnp.where(keep, 1.0, 0.0),)):
-            message = jnp.where(lane == rank + i, piece, message)
-        back_out[...] = message.astype(BF16)
-        backs.start()
-        for c, cols in enumerate(done_b):
-            normed = jnp.dot(back_scaled, down[:, cols], preferred_element_type=F32)
-            out_b[:, cols] = (
-                kept[:, cols].astype(F32)
-                + gain_ref[:, cols].astype(F32) * normed
-                - sav[:, cols].astype(F32) * tilt
-            ).astype(BF16)
-            shift(1, out_b, next_gr, c).start()
+            for g in range(2):
+                shift(0, out_f, next_in, g, c).start()
 
     def trade(i, k):
         target = (dp + k) % n_dp
@@ -336,10 +378,11 @@
         raw_savs.wait_recv()
         raw_grads.wait_recv()
         backs.wait_recv()
+        sides.wait_recv()
         came = back_in[...].astype(F32)
-        far_tilt = jnp.sum(jnp.where((lane == rank) | (lane == rank + 1), came, 0.0), axis=1, keepdims=True)
-        far_keep = jnp.sum(jnp.where(lane == rank + 2, came, 0.0), axis=1, keepdims=True)
-        far_back = came[:, :rank].astype(BF16)
+        far_back = jnp.concatenate([came[:, :rank], came[:, rank:]], axis=0).astype(BF16)
+        far_tilt = to_column(side_in[0:1])
+        far_keep = to_column(side_in[1:2])
         for a in range(0, raw_b, chunk):
             b = min(a + chunk, raw_b)
             cols = slice(width - raw_b + a, width - raw_b + b)
@@ -354,19 +397,19 @@
     def _():
         for copy in up_way:
             copy.wait_send()
-        for c in range(len(done_f)):
-            shift(0, out_f, next_in, c).wait_send()
-        for c in range(len(done_b)):
-            shift(1, out_b, next_gr, c).wait_recv()
+        for copy in shifts(0):
+            copy.wait_send()
+        for copy in shifts(1):
+            copy.wait_recv()
 
     @pl.when(sec > 0)
     def _():
         for copy in down_way:
             copy.wait_send()
-        for c in range(len(done_b)):
-            shift(1, out_b, next_gr, c).wait_send()
-        for c in range(len(done_f)):
-            shift(0, out_f, next_in, c).wait_recv()
+        for copy in shifts(1):
+            copy.wait_send()
+        for copy in shifts(0):
+            copy.wait_recv()
 
 
 def place(*refs):
@@ -391,7 +434,7 @@
         n_chunk = width // chunk
         raw_f = int(width * RAW_FORWARD) // LANES * LANES
         raw_b = int(width * RAW_BACK) // LANES * LANES
-        wide = -(-(rank + 4) // LANES) * LANES
+        peers = max(n_ten - 1, 1)
         steps = max(bits, 1)
         vmem = pl.BlockSpec(memory_space=pltpu.VMEM)
         anywhere = pl.BlockSpec(memory_space=pl.ANY)
@@ -410,10 +453,10 @@
                 pltpu.VMEM((rank, width), BF16),
                 pltpu.VMEM((rank, width), BF16),
                 pltpu.VMEM((rows, width), BF16),
-                pltpu.VMEM((rows, wide), F32),
+                pltpu.VMEM((rows, rank), F32),
                 pltpu.VMEM((rows, 2 * rank), F32),
-                pltpu.VMEM((steps, rows, wide), BF16),
-                pltpu.VMEM((steps, rows, wide), BF16),
+                pltpu.VMEM((steps, rows, rank), BF16),
+                pltpu.VMEM((steps, rows, rank), BF16),
                 pltpu.VMEM((steps, rows, 2 * rank), BF16),
                 pltpu.VMEM((steps, rows, 2 * rank), BF16),
                 pltpu.VMEM((rows, width), BF16),
@@ -422,8 +465,14 @@
                 pltpu.VMEM((2, max(n_dp - 1, 1), share, width), BF16),
                 pltpu.VMEM((rows // 2, 2 * rank), BF16),
                 pltpu.VMEM((rows // 2, 2 * rank), BF16),
-                pltpu.VMEM((rows, wide), BF16),
-                pltpu.VMEM((rows, wide), BF16),
+                pltpu.VMEM((rows // 2, 2 * rank), BF16),
+                pltpu.VMEM((rows // 2, 2 * rank), BF16),
+                pltpu.VMEM((8, rows), F32),
+                pltpu.VMEM((8, rows), F32),
+                pltpu.VMEM((2, 8, rows), F32),
+                pltpu.VMEM((2, peers, 8, rows), F32),
+                dma((2, peers)),
+                dma((2, peers)),
                 pltpu.VMEM((rows, raw_f), BF16),
                 pltpu.VMEM((rank, raw_f), BF16),
                 pltpu.VMEM((rows, raw_b), BF16),
@@ -433,14 +482,14 @@
                 dma((5,)),
                 dma((2, steps)),
                 dma((2, steps)),
-                dma((2, steps)),
-                dma((2, steps)),
-                dma((2, n_chunk)),
-                dma((2, n_chunk)),
+                dma((BLOCKS, steps)),
+                dma((BLOCKS, steps)),
+                dma((2, 2, n_chunk)),
+                dma((2, 2, n_chunk)),
                 dma((2, max(n_dp - 1, 1))),
                 dma((2, max(n_dp - 1, 1))),
-                dma((8,)),
-                dma((8,)),
+                dma((9,)),
+                dma((9,)),
                 dma((2, max(n_dp - 1, 1))),
                 dma((2, max(n_dp - 1, 1))),
             ],

time: 34.3 us -> 33.2 us (0.968)
  Pallas kernels: 33.4 us -> 32.3 us
    pallas_call x1, Pallas kernels: 32 us -> 30.9 us  [shards(): pl.pallas_call(functools.partial(tick, (n_sec, n_ten, n_dp, chunk)), out_...]
where the time goes in v4:
time: 33.2 us; the launch traced here: 32.9 us
  Pallas kernels  32.3 us (97%)
  between operations  0.64 us (2%)
    pallas_call x1, Pallas kernels, shards(): pl.pallas_call(functools.partial(tick, (n_sec, n_ten, n_dp, chunk)), out_...  30.9 us
    pallas_call x1, Pallas kernels, shards(): pl.pallas_call(place, out_shape=tuple((jax.ShapeDtypeStruct(shape, BF16)...  1.43 us

profile of v4, /device:TPU:0, one launch (start us, length us, event | category | flops | bytes accessed | tf_op | source)
XLA Modules:
  0.0 32.9 jit_solution(17782201929564729585)
XLA Ops:
  0.6 30.9 %tick.1 = (bf16[192,2048]{1,0:T(8,128)(2,1)S(1)}, bf16[192,2048]{1,0:T(8,128)(2,1)S(1)}, bf16[96,2048]{1,0:T(8,128)(2,1)S(1)}, bf16[96,2048]{1,0:T(8,128)(2,1)S(1)}) custom-call(bf16[192,2048]{1,0:T(8,128)(2,1)} %bitcast.10, bf16[192,2048]{1,0:T(8,128)(2,1)} %bitcast.11, bf16[192,2048]{1,0:T(8,128)(2,1)} %bitcast.12, s32[1,2]{1,0:T(1,128)} %bitcast.15, ...), custom_call_target="tpu_custom_call" | custom-call | flops 1056964608 | bytes 6291456 | tf_op jit(solution)/shard_map/tick/pallas_call | solution.py:444
  31.5 1.4 %place.1 = (bf16[192,2048]{1,0:T(8,128)(2,1)}, bf16[192,2048]{1,0:T(8,128)(2,1)}, bf16[96,2048]{1,0:T(8,128)(2,1)}, bf16[96,2048]{1,0:T(8,128)(2,1)}) custom-call(bf16[192,2048]{1,0:T(8,128)(2,1)S(1)} %get-tuple-element.12.refs_0_, bf16[192,2048]{1,0:T(8,128)(2,1)S(1)} %get-tuple-element.13.refs_1_, bf16[96,2048]{1,0:T(8,128)(2,1)S(1)} %get-tuple-element.14.refs_2_, ...), custom_call_target="tpu_custom_call" | custom-call | tf_op jit(solution)/shard_map/place/pallas_call | solution.py:504

commit v5 on v4

--- a/solution.py
+++ b/solution.py
@@ -9,8 +9,8 @@
 
 EPSILON = 1e-05
 LANES = 128
-RAW_FORWARD = 0.375
-RAW_BACK = 0.125
+RAW_FORWARD = 0.4375
+RAW_BACK = 0.1875
 BLOCKS = 4
 F32 = jnp.float32
 BF16 = jnp.bfloat16

time: 33.2 us -> 33.6 us (1.012)
  Pallas kernels: 32.3 us -> 32.7 us
    pallas_call x1, Pallas kernels: 30.9 us -> 31.3 us  [shards(): pl.pallas_call(functools.partial(tick, (n_sec, n_ten, n_dp, chunk)), out_...]
where the time goes in v5:
time: 33.6 us; the launch traced here: 33.3 us
  Pallas kernels  32.7 us (97%)
  between operations  0.64 us (2%)
    pallas_call x1, Pallas kernels, shards(): pl.pallas_call(functools.partial(tick, (n_sec, n_ten, n_dp, chunk)), out_...  31.3 us
    pallas_call x1, Pallas kernels, shards(): pl.pallas_call(place, out_shape=tuple((jax.ShapeDtypeStruct(shape, BF16)...  1.43 us

profile of v5, /device:TPU:0, one launch (start us, length us, event | category | flops | bytes accessed | tf_op | source)
XLA Modules:
  0.0 33.3 jit_solution(9705202087831584320)
XLA Ops:
  0.6 31.3 %tick.1 = (bf16[192,2048]{1,0:T(8,128)(2,1)S(1)}, bf16[192,2048]{1,0:T(8,128)(2,1)S(1)}, bf16[96,2048]{1,0:T(8,128)(2,1)S(1)}, bf16[96,2048]{1,0:T(8,128)(2,1)S(1)}) custom-call(bf16[192,2048]{1,0:T(8,128)(2,1)} %bitcast.10, bf16[192,2048]{1,0:T(8,128)(2,1)} %bitcast.11, bf16[192,2048]{1,0:T(8,128)(2,1)} %bitcast.12, s32[1,2]{1,0:T(1,128)} %bitcast.15, ...), custom_call_target="tpu_custom_call" | custom-call | flops 1056964608 | bytes 6291456 | tf_op jit(solution)/shard_map/tick/pallas_call | solution.py:444
  31.9 1.4 %place.1 = (bf16[192,2048]{1,0:T(8,128)(2,1)}, bf16[192,2048]{1,0:T(8,128)(2,1)}, bf16[96,2048]{1,0:T(8,128)(2,1)}, bf16[96,2048]{1,0:T(8,128)(2,1)}) custom-call(bf16[192,2048]{1,0:T(8,128)(2,1)S(1)} %get-tuple-element.12.refs_0_, bf16[192,2048]{1,0:T(8,128)(2,1)S(1)} %get-tuple-element.13.refs_1_, bf16[96,2048]{1,0:T(8,128)(2,1)S(1)} %get-tuple-element.14.refs_2_, ...), custom_call_target="tpu_custom_call" | custom-call | tf_op jit(solution)/shard_map/place/pallas_call | solution.py:504
